TPU v7x, 256 devices: a whole 4x4x8 slice. The times are simulated.
256 devices in a mesh: phase: 16 (over y, x), line: 16 (over z, core).
Axes of the slice: x: 4, y: 4, z: 8, core: 2. Of those that a mesh axis runs over, the one named last changes fastest.
Arguments:
- signal: bfloat16 [16, 16, 8192, 256], P('phase', 'line'), may hold values from -8 to 8, as said below
- tap_gain: float32 [3, 256], replicated, may hold values from 0.3 to 1.2
Outputs:
- echoed: bfloat16 [16, 16, 8192, 256], P('phase', 'line')
Inputs may be any that keep to these rules, and one draw needn't show every extreme that they name: signal holds numbers from -8 to 8.
All inputs are finite; a program needn't handle non-finite values.
Results may differ from a plain program's by a relative error of at most 0.0055.
Values may be sent and summed in bfloat16 or wider, within the bound.
No kernel may reach another device: no remote copies, remote signals or barrier semaphores. Data moves between devices by JAX's collectives and lax.ppermute only.
A program may use at most 64 MiB of HBM per device.

v0:
```python
import jax
import jax.numpy as jnp
from jax import lax
from jax.sharding import Mesh
from jax.sharding import PartitionSpec as P

PHASE = ("phase_0", "phase_1")


def cut_along(array, dim, peers):
    shape = array.shape
    pieces = array.reshape(*shape[:dim], peers, shape[dim] // peers, *shape[dim + 1 :])
    return jnp.moveaxis(pieces, dim, 0)


def cut_rows(length, count):
    unit = 8 if length >= 8 * count else 1
    return [length // unit * k // count * unit for k in range(1, count)]


def laid_out(pieces, dim):
    shape = list(pieces.shape[1:])
    shape[dim] *= pieces.shape[0]
    return jnp.moveaxis(pieces, 0, dim).reshape(shape)


def exchange_in_pieces(array, axis, pieces, split_dim, concat_dim):
    blocks = cut_along(array, split_dim, lax.axis_size(axis))
    split_at = max(range(1, max(2, blocks.ndim - 1)), key=lambda d: blocks.shape[d])
    outs = []
    for share in jnp.split(blocks, cut_rows(blocks.shape[split_at], pieces), axis=split_at):
        if share.size:
            outs.append(lax.all_to_all(share, axis, split_axis=0, concat_axis=0, tiled=True))
    return laid_out(jnp.concatenate(outs, axis=split_at), concat_dim)


def by_axis(array, axes):
    for axis in axes:
        array = lax.psum(array, axis)
    return array


def body(signal, tap_gain):
    all_segments = exchange_in_pieces(signal, PHASE, 2, 2, 0).astype(jnp.float32)
    summed = (
        tap_gain[0] * all_segments
        + tap_gain[1] * jnp.roll(all_segments, 2, axis=0)
        + tap_gain[2] * jnp.roll(all_segments, 3, axis=0)
    )
    power = by_axis(jnp.sum(summed * summed, axis=(0, 2), keepdims=True), PHASE) / (
        signal.shape[2] * lax.axis_size(PHASE)
    )
    echoed = (summed * lax.rsqrt(power + 1e-05)).astype(jnp.bfloat16)
    echoed = lax.all_to_all(echoed, PHASE, split_axis=0, concat_axis=2, tiled=True)
    return echoed


def solution(mesh):
    finer = Mesh(mesh.devices.reshape(4, 4, mesh.shape["line"]), ("phase_0", "phase_1", "line"))
    return jax.shard_map(
        body,
        mesh=finer,
        in_specs=(P(PHASE, "line", None, None), P()),
        out_specs=P(PHASE, "line", None, None),
        check_vma=False,
    )
```

profile of v0, /device:TPU:66, one launch (start us, length us, event | category | flops | bytes accessed | tf_op | source)
XLA Modules:
  0.0 167.8 jit_solution(15783933608181015372)
XLA Ops:
  0.0 0.0 copy-start.2
  0.0 4.0 %fusion.5 = (bf16[16,1,1,256,256]{4,3,2,1,0:T(8,128)(2,1)S(1)}, bf16[16,1,1,256,256]{4,3,2,1,0:T(8,128)(2,1)}) fusion(bf16[16,1,1,512,256]{4,3,2,1,0:T(8,128)(2,1)} %bitcast.25), kind=kLoop, calls=%fused_computation.15 | loop fusion | bytes 8388608 | tf_op jit(solution)/shard_map/split | solution.py:31
  4.0 35.3 %all_to_all.22 = bf16[16,1,1,256,256]{4,3,2,1,0:T(8,128)(2,1)} all-to-all(bf16[16,1,1,256,256]{4,3,2,1,0:T(8,128)(2,1)S(1)} %get-tuple-element.9), channel_id=1, replica_groups=mesh['phase_0'=4,'phase_1'=4,'line'=16] {'phase_0','phase_1'}, dimensions={0} | all-to-all | bytes 4194304 | tf_op jit(solution)/shard_map/all_to_all | solution.py:33
  39.3 5.3 %all-to-all-start.1 = ((bf16[16,1,1,256,256]{4,3,2,1,0:T(8,128)(2,1)}), bf16[16,1,1,256,256]{4,3,2,1,0:T(8,128)(2,1)}, u32[]{:S(2)}, u32[]{:S(2)}) async-start(bf16[16,1,1,256,256]{4,3,2,1,0:T(8,128)(2,1)} %get-tuple-element.10), calls=%async_computation.1 | async-start | bytes 4194304 | tf_op jit(solution)/shard_map/all_to_all | solution.py:33
  44.6 0.0 copy-done.2
  44.6 29.3 %all-to-all-done.1 = bf16[16,1,1,256,256]{4,3,2,1,0:T(8,128)(2,1)} async-done(((bf16[16,1,1,256,256]{4,3,2,1,0:T(8,128)(2,1)}), bf16[16,1,1,256,256]{4,3,2,1,0:T(8,128)(2,1)}, u32[]{:S(2)}, u32[]{:S(2)}) %all-to-all-start.1) | async-done | bytes 2097184 | tf_op jit(solution)/shard_map/all_to_all | solution.py:33
  73.9 6.6 %fusion.3 = (f32[16,1,1,512,256]{4,3,0,2,1:T(8,128)S(1)}, f32[16,1,1,512,256]{4,3,2,1,0:T(8,128)}) fusion(bf16[16,1,1,256,256]{4,3,2,1,0:T(8,128)(2,1)} %all-to-all-done.1, bf16[16,1,1,256,256]{4,3,2,1,0:T(8,128)(2,1)} %all_to_all.22), kind=kLoop, calls=%fused_computation.12 | loop fusion | flops 8388608 | bytes 20971520 | tf_op jit(solution)/shard_map/convert_element_type | solution.py:44
  80.5 0.1 slice_bitcast_fusion.3
  80.5 1.2 slice_bitcast_fusion.2
  81.8 0.8 slice_bitcast_fusion
  82.6 0.0 copy-start
  82.6 0.0 copy-start.1
  82.6 3.5 %slice_bitcast_fusion.1 = f32[13,1,512,256]{3,2,0,1:T(8,128)S(1)} fusion(f32[16,1,1,512,256]{4,3,2,1,0:T(8,128)} %get-tuple-element.8), kind=kLoop, calls=%fused_computation.8 | loop fusion | bytes 13631488 | tf_op jit(solution)/shard_map/jit(_roll_static)/slice | solution.py:48
  86.2 0.0 copy-done
  86.2 0.4 copy-done.1
  86.6 5.6 %multiply_reduce_fusion = (f32[256]{0:T(256)S(1)}, f32[16,1,512,256]{3,2,0,1:T(8,128)}) fusion(f32[13,1,512,256]{3,2,0,1:T(8,128)S(1)} %slice_bitcast_fusion.1, f32[3,1,512,256]{3,2,0,1:T(8,128)S(1)} %copy-done.1, f32[256]{0:T(256)S(1)} %bitcast.29, f32[14,1,512,256]{3,2,0,1:T(8,128)S(1)} %slice_bitcast_fusion, ...), kind=kLoop, calls=%fused_computation.6 | loop fusion | flops 27262720 | bytes 29364224 | tf_op jit(solution)/shard_map/reduce_sum | solution.py:50
  92.3 8.7 %psum.14 = f32[1,1,1,256]{3,2,1,0:T(1,128)S(1)} all-reduce(f32[1,1,1,256]{3,2,1,0:T(1,128)S(1)} %bitcast.26), channel_id=1, replica_groups=mesh['phase_0'=4,'phase_1'=4,'line'=16] {'phase_0'}, use_global_device_ids=true, to_apply=%region_1.2 | all-reduce | flops 256 | bytes 2048 | tf_op jit(solution)/shard_map/psum | solution.py:39
  101.0 9.3 %psum.15 = f32[1,1,1,256]{3,2,1,0:T(1,128)S(1)} all-reduce(f32[1,1,1,256]{3,2,1,0:T(1,128)S(1)} %psum.14), channel_id=1, replica_groups=mesh['phase_0'=4,'phase_1'=4,'line'=16] {'phase_1'}, use_global_device_ids=true, to_apply=%region_2.3 | all-reduce | flops 256 | bytes 2048 | tf_op jit(solution)/shard_map/psum | solution.py:39
  110.3 4.2 %fusion.2 = bf16[16,1,512,256]{3,2,1,0:T(8,128)(2,1)S(1)} fusion(f32[16,1,512,256]{3,2,0,1:T(8,128)} %get-tuple-element.6, f32[256]{0:T(256)S(1)} %bitcast.27), kind=kLoop, calls=%fused_computation.9 | loop fusion | flops 4194304 | bytes 12583936 | tf_op jit(solution)/shard_map/convert_element_type | solution.py:53
  114.5 51.3 %all_to_all.23 = bf16[16,1,512,256]{3,2,1,0:T(8,128)(2,1)S(1)} all-to-all(bf16[16,1,512,256]{3,2,1,0:T(8,128)(2,1)S(1)} %fusion.2), channel_id=1, replica_groups=mesh['phase_0'=4,'phase_1'=4,'line'=16] {'phase_0','phase_1'}, dimensions={0} | all-to-all | bytes 8388608 | tf_op jit(solution)/shard_map/all_to_all | solution.py:54
  165.8 2.0 %copy.8 = bf16[1,1,8192,256]{3,2,1,0:T(8,128)(2,1)} copy(bf16[1,1,8192,256]{3,2,1,0:T(8,128)(2,1)S(1)} %bitcast.24) | data formatting | bytes 8388608
  (2 shorter events, 0.0 us)
Async XLA Ops:
  0.0 44.6 %copy-start.2 = (f32[3,256]{1,0:T(4,128)S(1)}, f32[3,256]{1,0:T(4,128)}, u32[]{:S(2)}) copy-start(f32[3,256]{1,0:T(4,128)} %param.3) | copy-start | bytes 9220
  39.3 34.6 %all-to-all-start.1 = ((bf16[16,1,1,256,256]{4,3,2,1,0:T(8,128)(2,1)}), bf16[16,1,1,256,256]{4,3,2,1,0:T(8,128)(2,1)}, u32[]{:S(2)}, u32[]{:S(2)}) async-start(bf16[16,1,1,256,256]{4,3,2,1,0:T(8,128)(2,1)} %get-tuple-element.10), calls=%async_computation.1 | async-start | bytes 4194304 | tf_op jit(solution)/shard_map/all_to_all | solution.py:33
  82.6 3.6 %copy-start = (bf16[16,1,1,256,256]{4,3,2,1,0:T(8,128)(2,1)S(1)}, bf16[16,1,1,256,256]{4,3,2,1,0:T(8,128)(2,1)}, u32[]{:S(2)}) copy-start(bf16[16,1,1,256,256]{4,3,2,1,0:T(8,128)(2,1)} %all_to_all.22) | copy-start | bytes 6291460
  82.6 4.0 %copy-start.1 = (f32[3,1,512,256]{3,2,0,1:T(8,128)S(1)}, f32[3,1,512,256]{3,2,0,1:T(8,128)}, u32[]{:S(2)}) copy-start(f32[3,1,512,256]{3,2,0,1:T(8,128)} %slice_bitcast_fusion.2) | copy-start | bytes 4718596
where the time goes:
time: 168 us
  blocking collectives  105 us (62%)
  waiting for transfers between devices  29.3 us (17%)
  other arithmetic  16.5 us (10%)
  local copies, waits for them, and re-layouts  12.1 us (7%)
  starting transfers between devices  5.3 us (3%)
    all_to_all x1, blocking collectives, body(): lax.all_to_all(echoed, PHASE, split_axis=0, concat_axis=2, tiled=True)  51.3 us
    all_to_all x1, blocking collectives, exchange_in_pieces(): lax.all_to_all(share, axis, split_axis=0, concat_axis=0, tiled=True)  35.3 us
    all_to_all x1, waiting for transfers between devices, exchange_in_pieces(): lax.all_to_all(share, axis, split_axis=0, concat_axis=0, tiled=True)  29.3 us
    psum x2, blocking collectives, by_axis(): array = lax.psum(array, axis)  18 us
    convert_element_type x1, other arithmetic, body(): exchange_in_pieces(signal, PHASE, 2, 2, 0).astype(jnp.float32)  6.56 us
    reduce_sum x1, other arithmetic, body(): jnp.sum(summed * summed, axis=(0, 2), keepdims=True)  5.65 us
    all_to_all x1, starting transfers between devices, exchange_in_pieces(): lax.all_to_all(share, axis, split_axis=0, concat_axis=0, tiled=True)  5.3 us
    slice x2, local copies, waits for them, and re-layouts, body(): jnp.roll(all_segments, 3, axis=0)  4.79 us
  transfers between devices with their start and end apart: 1, of which 1 were waited for; matrix products, arithmetic and copies ran while one was open for 0% of the time, Pallas kernels for 0%

commit v1 on v0

v1 whole, which is shorter than its diff:
```python
import jax
import jax.numpy as jnp
from jax import lax
from jax.experimental import pallas as pl
from jax.experimental.pallas import tpu as pltpu
from jax.sharding import PartitionSpec as P

TILE = 16
EXTRA = 16
VMEM = 24 * 1024 * 1024


def mix_kernel(chunk_ref, gain_ref, mixed_ref):
    segments, rows, channels = chunk_ref.shape
    g0, g1, g2 = (jnp.broadcast_to(gain_ref[k : k + 1, :], (TILE, channels)) for k in range(3))

    def step(i, total):
        at = pl.ds(pl.multiple_of(i * TILE, TILE), TILE)
        wide = [chunk_ref[s, at, :].astype(jnp.float32) for s in range(segments)]
        for s in range(segments):
            mixed = g0 * wide[s] + g1 * wide[s - 2] + g2 * wide[s - 3]
            mixed_ref[s, at, :] = mixed.astype(jnp.bfloat16)
            total = total + mixed * mixed
        return total

    total = lax.fori_loop(0, rows // TILE, step, jnp.zeros((TILE, channels), jnp.float32))
    power = jnp.sum(total, axis=0, keepdims=True)
    high = power.astype(jnp.bfloat16)
    rest = power - high.astype(jnp.float32)
    middle = rest.astype(jnp.bfloat16)
    low = (rest - middle.astype(jnp.float32)).astype(jnp.bfloat16)
    row = lax.broadcasted_iota(jnp.int32, (EXTRA, channels), 0)
    spread = lambda a: jnp.broadcast_to(a.astype(jnp.float32), (EXTRA, channels))
    terms = jnp.where(
        row == 0,
        spread(high),
        jnp.where(row == 1, spread(middle), jnp.where(row == 2, spread(low), 0.0)),
    ).astype(jnp.bfloat16)
    for s in range(segments):
        mixed_ref[s, pl.ds(rows, EXTRA), :] = terms


def mix(chunk, tap_gain):
    segments, rows, channels = chunk.shape
    return pl.pallas_call(
        mix_kernel,
        in_specs=[pl.BlockSpec(memory_space=pltpu.VMEM)] * 2,
        out_specs=pl.BlockSpec(memory_space=pltpu.VMEM),
        out_shape=jax.ShapeDtypeStruct((segments, rows + EXTRA, channels), jnp.bfloat16),
        cost_estimate=pl.CostEstimate(
            flops=10 * chunk.size, bytes_accessed=4 * chunk.size, transcendentals=0
        ),
        compiler_params=pltpu.CompilerParams(vmem_limit_bytes=VMEM),
        name="mix",
    )(chunk, tap_gain)


def scale_kernel(count, mixed_ref, out_ref, held, sems):
    segments, rows, channels = mixed_ref.shape
    rows -= EXTRA
    power = jnp.zeros((EXTRA, channels), jnp.float32)
    for s in range(segments):
        power = power + mixed_ref[s, pl.ds(rows, EXTRA), :].astype(jnp.float32)
    power = jnp.sum(power, axis=0, keepdims=True) / count
    scale = jnp.broadcast_to(lax.rsqrt(power + 1e-05), (TILE, channels))
    copies = []
    for s in range(segments):

        def step(i, carry):
            at = pl.ds(pl.multiple_of(i * TILE, TILE), TILE)
            held[s, at, :] = (mixed_ref[s, at, :].astype(jnp.float32) * scale).astype(jnp.bfloat16)
            return carry

        lax.fori_loop(0, rows // TILE, step, 0, unroll=4)
        copies.append(
            pltpu.make_async_copy(held.at[s], out_ref.at[pl.ds(s * rows, rows)], sems.at[s])
        )
        copies[-1].start()
    for copy in copies:
        copy.wait()


def scale(mixed, count):
    segments, rows, channels = mixed.shape
    rows -= EXTRA
    size = segments * rows * channels
    return pl.pallas_call(
        lambda *refs: scale_kernel(count, *refs),
        in_specs=[pl.BlockSpec(memory_space=pltpu.VMEM)],
        out_specs=pl.BlockSpec(memory_space=pl.ANY),
        out_shape=jax.ShapeDtypeStruct((segments * rows, channels), jnp.bfloat16),
        scratch_shapes=[
            pltpu.VMEM((segments, rows, channels), jnp.bfloat16),
            pltpu.SemaphoreType.DMA((segments,)),
        ],
        cost_estimate=pl.CostEstimate(flops=2 * size, bytes_accessed=4 * size, transcendentals=0),
        compiler_params=pltpu.CompilerParams(vmem_limit_bytes=VMEM),
        name="scale",
    )(mixed)


def body(signal, tap_gain):
    steps, channels = signal.shape[2:]
    peers = lax.axis_size("phase")
    pieces = signal.reshape(peers, steps // peers, channels)
    arrived = lax.all_to_all(pieces, "phase", split_axis=0, concat_axis=0, tiled=True)
    mixed = mix(arrived, tap_gain)
    home = lax.all_to_all(mixed, "phase", split_axis=0, concat_axis=0, tiled=True)
    return scale(home, steps * peers).reshape(signal.shape)


def solution(mesh):
    return jax.shard_map(
        body,
        mesh=mesh,
        in_specs=(P("phase", "line", None, None), P()),
        out_specs=P("phase", "line", None, None),
        check_vma=False,
    )
```

time: 168 us -> 124 us (0.74); the launches traced: 168 us -> 122 us
  waiting for transfers between devices: 29.3 us -> 0 us
  other arithmetic: 16.5 us -> 0 us
  local copies, waits for them, and re-layouts: 12.1 us -> 0.01 us
  blocking collectives: 105 us -> 117 us
  starting transfers between devices: 5.3 us -> 0 us
  Pallas kernels: 0 us -> 4.7 us
    all_to_all x2, blocking collectives: 86.6 us -> 117 us  [the longest x1 60.5 us: body(): lax.all_to_all(pieces, 'phase', split_axis=0, concat_axis=0, tiled=True)]
    all_to_all x1 -> x0, waiting for transfers between devices: 29.3 us -> none  [exchange_in_pieces(): lax.all_to_all(share, axis, split_axis=0, concat_axis=0, tiled=True)]
    psum x2 -> x0, blocking collectives: 18 us -> none  [by_axis(): array = lax.psum(array, axis)]
    convert_element_type x2 -> x0, other arithmetic: 10.8 us -> none  [the longest x1 6.56 us: body(): exchange_in_pieces(signal, PHASE, 2, 2, 0).astype(jnp.float32)]
    slice x5 -> x0, local copies, waits for them, and re-layouts: 5.71 us -> none  [the longest x2 4.79 us: body(): jnp.roll(all_segments, 3, axis=0)]
    reduce_sum x1 -> x0, other arithmetic: 5.65 us -> none  [body(): jnp.sum(summed * summed, axis=(0, 2), keepdims=True)]
    all_to_all x1 -> x0, starting transfers between devices: 5.3 us -> none  [exchange_in_pieces(): lax.all_to_all(share, axis, split_axis=0, concat_axis=0, tiled=True)]
    pallas_call x0 -> x2, Pallas kernels: none -> 4.7 us  [the longest x1 2.46 us: mix(): pl.pallas_call(mix_kernel, in_specs=[pl.BlockSpec(memory_space=pltpu.VMEM...]
  transfers between devices with their start and end apart: 1 -> 0, of which waited for: 1 -> 0; matrix products, arithmetic and copies ran while one was open for 0% -> 0% of each run, Pallas kernels for 0% -> 0%
where the time goes in v1:
time: 124 us; the launch traced here: 122 us
  blocking collectives  117 us (94%)
  Pallas kernels  4.7 us (4%)
    all_to_all x1, blocking collectives, body(): lax.all_to_all(pieces, 'phase', split_axis=0, concat_axis=0, tiled=True)  60.5 us
    all_to_all x1, blocking collectives, body(): lax.all_to_all(mixed, 'phase', split_axis=0, concat_axis=0, tiled=True)  56.7 us

profile of v1, /device:TPU:66, one launch (start us, length us, event | category | flops | bytes accessed | tf_op | source)
XLA Modules:
  0.0 121.8 jit_solution(12712616498041455680)
XLA Ops:
  0.0 0.0 copy-start
  0.0 60.5 %all_to_all.10.chunk_ref = bf16[16,512,256]{2,1,0:T(8,128)(2,1)S(1)} all-to-all(bf16[16,512,256]{2,1,0:T(8,128)(2,1)} %bitcast.2), channel_id=1, replica_groups=mesh['phase'=16,'line'=16] {'phase'}, dimensions={0} | all-to-all | bytes 8388608 | tf_op jit(solution)/shard_map/all_to_all | solution.py:106
  60.5 0.0 copy-done
  60.5 2.5 %mix.1 = bf16[16,528,256]{2,1,0:T(8,128)(2,1)S(1)} custom-call(bf16[16,512,256]{2,1,0:T(8,128)(2,1)S(1)} %all_to_all.10.chunk_ref, f32[3,256]{1,0:T(4,128)S(1)} %copy-done), custom_call_target="tpu_custom_call" | custom-call | flops 20971520 | bytes 8388608 | tf_op jit(solution)/shard_map/mix/pallas_call | solution.py:45
  63.0 56.7 %all_to_all.11.refs_0_ = bf16[16,528,256]{2,1,0:T(8,128)(2,1)S(1)} all-to-all(bf16[16,528,256]{2,1,0:T(8,128)(2,1)S(1)} %mix.1), channel_id=1, replica_groups=mesh['phase'=16,'line'=16] {'phase'}, dimensions={0} | all-to-all | bytes 8650752 | tf_op jit(solution)/shard_map/all_to_all | solution.py:108
  119.6 2.2 %scale.1 = bf16[8192,256]{1,0:T(8,128)(2,1)} custom-call(bf16[16,528,256]{2,1,0:T(8,128)(2,1)S(1)} %all_to_all.11.refs_0_), custom_call_target="tpu_custom_call" | custom-call | flops 4194304 | bytes 8388608 | tf_op jit(solution)/shard_map/scale/pallas_call | solution.py:87
Async XLA Ops:
  0.0 60.5 %copy-start = (f32[3,256]{1,0:T(4,128)S(1)}, f32[3,256]{1,0:T(4,128)}, u32[]{:S(2)}) copy-start(f32[3,256]{1,0:T(4,128)} %gain_ref.1) | copy-start | bytes 9220
